TPU v7x, 32 devices: a whole 2x2x4 slice. The times are simulated.
32 devices in a mesh: dp: 8 (over z, x), tensor: 4 (over y, core).
Axes of the slice: x: 2, y: 2, z: 4, core: 2. Of those that a mesh axis runs over, the one named last changes fastest.
Arguments:
- hidden: bfloat16 [2048, 14336], P('dp', 'tensor'), parts along dimension 0, may hold values from -16 to 16
- signs: int32 [14336], P('tensor'), may hold values 0 or 1
- packed: int32 [14336, 512], P('tensor'), may hold values from -2147483648 to 2147483646
- group_scales: int32 [112, 4096], P('tensor'), may hold values from 1 to 16
- residual: bfloat16 [2048, 4096], P(('dp', 'tensor')), parts along dimension 0, may hold values from -16 to 16
Outputs:
- new_residual: bfloat16 [2048, 4096], P(('dp', 'tensor')), parts along dimension 0
- normed: bfloat16 [2048, 4096], P(('dp', 'tensor')), parts along dimension 0
There are 8 independent parts, one for each index of `dp`. A program takes and returns all parts, laid end to end along the dimension named above; an argument that names none is the same for every part. Nothing has to cross between parts.
Inputs may be any that keep to these rules, and one draw needn't show every extreme that they name: `packed`: bits 4 k to 4 k + 3 of word j in row f hold the code of output feature k * 512 + j plus 8.
All inputs are finite; a program needn't handle non-finite values. No bound on the sum of `signs` on one device may be relied on, other than what follows from the above.
Results may differ from a plain program's by a relative error of at most 0.0054.
Values may be sent and summed in bfloat16 or wider, within the bound.
No kernel may reach another device: no remote copies, remote signals or barrier semaphores. Data moves between devices by JAX's collectives and lax.ppermute only.
A program may use at most 256 MiB of HBM per device.

v0:
```python
import functools
import math

import jax
import jax.numpy as jnp
import numpy as np
from jax import lax
from jax.experimental import pallas as pl
from jax.experimental.pallas import tpu as pltpu
from jax.sharding import PartitionSpec as P


ORDER = 28
DENSE = 896
TILE_ROWS = 16
VMEM = pl.BlockSpec(memory_space=pltpu.VMEM)
SMEM = pl.BlockSpec(memory_space=pltpu.SMEM)
HBM = pl.BlockSpec(memory_space=pltpu.HBM)
BYTES = 4
GRANT = 16


def chunk_rows(token_rows):
    quarter = token_rows // 4
    if quarter % TILE_ROWS:
        return [token_rows]
    return [quarter, 2 * quarter, quarter]


def paley_table():
    offsets = (np.arange(13)[None, :] - np.arange(13)[:, None]) % 13
    residues = np.zeros(13)
    residues[np.arange(1, 13) ** 2 % 13] = 1.0
    quadratic = np.where(offsets == 0, 0.0, np.where(residues[offsets] > 0, 1.0, -1.0))
    conference = np.zeros((14, 14))
    conference[0, 1:] = 1.0
    conference[1:, 0] = 1.0
    conference[1:, 1:] = quadratic
    upper = np.array([[1.0, 1.0], [1.0, -1.0]])
    lower = np.array([[1.0, -1.0], [-1.0, -1.0]])
    return np.kron(conference, upper) + np.kron(np.eye(14), lower)


def sylvester(order):
    table = np.ones((1, 1))
    while table.shape[0] < order:
        table = np.kron(np.array([[1.0, 1.0], [1.0, -1.0]]), table)
    return table


def cost(flops):
    return pl.CostEstimate(flops=flops, bytes_accessed=0, transcendentals=0)


def dense_table():
    return np.kron(sylvester(DENSE // ORDER), paley_table().T)


def bit_reversed(groups):
    bits = groups.bit_length() - 1
    return [sum(((d >> b) & 1) << (bits - 1 - b) for b in range(bits)) for d in range(groups)]


def sign_of(bit):
    return (1 - 2 * bit).astype(jnp.float32)


def flips_of(signs):
    return (2 * signs - 1).astype(jnp.float32).reshape(1, signs.shape[0])


def open_kernel(groups, token_rows, size, hidden_ref, signs_ref, out_ref, staged, flips, sems):
    copies = [pltpu.make_async_copy(signs_ref, flips, sems.at[groups])]
    for place, owner in enumerate(bit_reversed(groups)):
        copies.append(
            pltpu.make_async_copy(
                hidden_ref.at[pl.ds(owner * token_rows, size), :],
                staged.at[pl.ds(place * size, size), :],
                sems.at[place],
            )
        )
    for copy in copies:
        copy.start()
    for copy in copies:
        copy.wait()
    out_ref[...] = (staged[...].astype(jnp.float32) * flips_of(flips[...])).astype(jnp.bfloat16)


def open_exchange(hidden, signs, groups, size):
    rows, width = groups * size, hidden.shape[1]
    return pl.pallas_call(
        functools.partial(open_kernel, groups, hidden.shape[0] // groups, size),
        out_shape=jax.ShapeDtypeStruct((rows, width), jnp.bfloat16),
        in_specs=[HBM, HBM],
        out_specs=VMEM,
        scratch_shapes=[
            pltpu.VMEM((rows, width), jnp.bfloat16),
            pltpu.VMEM((width,), jnp.int32),
            pltpu.SemaphoreType.DMA((groups + 1,)),
        ],
        compiler_params=pltpu.CompilerParams(vmem_limit_bytes=8 * 2**20),
        cost_estimate=cost(rows * width),
        name="open_exchange",
    )(*[pltpu.with_memory_space_constraint(value, pltpu.HBM) for value in (hidden, signs)])


def rotate_blocks(mixed, table_ref, stacked_ref):
    rows = mixed[0].shape[0]
    blocks = len(mixed)
    span = 1
    while span < blocks:
        for first in range(blocks):
            if not first & span:
                a, b = mixed[first], mixed[first + span]
                mixed[first], mixed[first + span] = a + b, a - b
        span *= 2
    for block in range(blocks):
        stacked_ref[pl.ds(block * rows, rows), :] = mixed[block].astype(jnp.bfloat16)
    turned = jnp.dot(stacked_ref[...], table_ref[...], preferred_element_type=jnp.float32)
    return [turned[block * rows : (block + 1) * rows] for block in range(blocks)]


def rotate_kernel(groups, places, me_ref, hidden_ref, signs_ref, other_ref, other_signs_ref, table_ref, *refs):
    first_ref, out_refs, stacked_ref = refs[0], refs[1:-1], refs[-1]
    width = hidden_ref.shape[1]
    token_rows = hidden_ref.shape[0] // groups
    flips = flips_of(signs_ref[...]) * sign_of(me_ref[0] & 1)
    other_flips = flips_of(other_signs_ref[...])

    def gather(ref, chosen, columns):
        rows = [
            ref[pl.ds(owner * token_rows + start, size), columns]
            for start, size in chosen
            for owner in bit_reversed(groups)
        ]
        return jnp.concatenate(rows, axis=0).astype(jnp.float32)

    mixed = []
    for block in range(width // DENSE):
        columns = pl.ds(block * DENSE, DENSE)
        flip = flips[:, block * DENSE : (block + 1) * DENSE]
        other_flip = other_flips[:, block * DENSE : (block + 1) * DENSE]
        first = gather(other_ref, places[:1], columns) * other_flip
        first_ref[:, columns] = first.astype(jnp.bfloat16)
        own = gather(hidden_ref, places[1:], columns) * flip
        mixed.append(own + gather(other_ref, places[1:], columns) * other_flip)
    for block, value in enumerate(rotate_blocks(mixed, table_ref, stacked_ref)):
        columns = pl.ds(block * DENSE, DENSE)
        start = 0
        for chunk, (_, size) in enumerate(places[1:]):
            piece = value[start : start + groups * size]
            start += groups * size
            out_refs[2 * chunk][:, columns] = piece
            out_refs[2 * chunk + 1][:, columns] = piece.astype(jnp.bfloat16)


def rotate(hidden, signs, other, other_signs, me, table, groups, places):
    width = hidden.shape[1]
    shapes = [jax.ShapeDtypeStruct((groups * places[0][1], width), jnp.bfloat16)]
    for _, size in places[1:]:
        shapes.append(jax.ShapeDtypeStruct((groups * size, width), jnp.float32))
        shapes.append(jax.ShapeDtypeStruct((groups * size, width), jnp.bfloat16))
    rows = groups * sum(size for _, size in places[1:])
    return pl.pallas_call(
        functools.partial(rotate_kernel, groups, places),
        out_shape=shapes,
        in_specs=[SMEM] + [VMEM] * 5,
        out_specs=[VMEM] * len(shapes),
        scratch_shapes=[pltpu.VMEM((rows * width // DENSE, DENSE), jnp.bfloat16)],
        compiler_params=pltpu.CompilerParams(vmem_limit_bytes=20 * 2**20),
        cost_estimate=cost(2 * rows * width * DENSE),
        name="rotate",
    )(me, hidden, signs, other, other_signs, pltpu.with_memory_space_constraint(table, pltpu.HBM))


def dequantize_kernel(packed_ref, bytes_ref):
    word = packed_ref[...] ^ np.int32(-2139062144)
    for place in range(BYTES):
        moved = jnp.right_shift(jnp.left_shift(word, 24 - 8 * place), 24)
        bytes_ref[place, :, :] = moved.astype(jnp.int8)


def dequantize(packed, group_count):
    width, words = packed.shape
    rows = width // group_count * 7 if group_count % 7 == 0 else width // group_count
    return pl.pallas_call(
        dequantize_kernel,
        grid=(width // rows,),
        out_shape=jax.ShapeDtypeStruct((BYTES, width, words), jnp.int8),
        in_specs=[pl.BlockSpec((rows, words), lambda i: (i, 0))],
        out_specs=pl.BlockSpec((BYTES, rows, words), lambda i: (0, i, 0)),
        compiler_params=pltpu.CompilerParams(vmem_limit_bytes=16 * 2**20),
        cost_estimate=cost(width * words * 8 * 512),
        name="dequantize",
    )(pltpu.with_memory_space_constraint(packed, pltpu.HBM))


def project_kernel(count, unit, rotate_first, me_ref, *refs):
    parts, refs = refs[:count], refs[count:]
    if rotate_first:
        table_ref, refs = refs[0], refs[1:]
    scales_ref, bytes_ref, keep_ref, send_ref, rotated_ref, stacked_ref = refs
    rows, width = parts[0].shape
    words = bytes_ref.shape[2]
    group_count = scales_ref.shape[0]
    group_size = width // group_count
    blocks = width // DENSE
    me = me_ref[0]
    signs = []
    for r in range(count):
        bits = me & (me ^ r) if rotate_first else jnp.right_shift(me, 1) & (1 - r)
        parity = bits & 1
        for shift in range(1, max(count.bit_length() - 1, 1)):
            parity = parity ^ (jnp.right_shift(bits, shift) & 1)
        signs.append(sign_of(parity))
    mixed = []
    for block in range(blocks):
        columns = pl.ds(block * DENSE, DENSE)
        total = signs[0] * parts[0][:, columns].astype(jnp.float32)
        for r in range(1, count):
            total = total + signs[r] * parts[r][:, columns].astype(jnp.float32)
        mixed.append(total)
    if rotate_first:
        mixed = rotate_blocks(mixed, table_ref, stacked_ref)
    for block in range(blocks):
        rotated_ref[:, pl.ds(block * DENSE, DENSE)] = (mixed[block] * unit).astype(jnp.bfloat16)
    half = rows // 2
    upper = me & 1 == 1

    @pl.loop(0, BYTES, unroll=2)
    def _(place):
        spans = [
            pl.ds(pl.multiple_of((2 * place + side) * words, words), words) for side in range(2)
        ]
        sides = [[], []]
        for group in range(group_count):
            both = bytes_ref[place, group * group_size : (group + 1) * group_size, :]
            high = (both & jnp.int8(-16)).astype(jnp.bfloat16)
            low = both.astype(jnp.bfloat16) - high - jnp.bfloat16(8)
            sides[0].append(low * scales_ref[group : group + 1, spans[0]])
            sides[1].append(high * scales_ref[group : group + 1, spans[1]])
        for columns, weights in zip(spans, sides):
            product = jnp.dot(
                rotated_ref[...],
                jnp.concatenate(weights, axis=0),
                preferred_element_type=jnp.float32,
            )
            first, second = product[:half], product[half:]
            keep_ref[:, columns] = jnp.where(upper, second, first)
            send_ref[:, columns] = jnp.where(upper, first, second).astype(jnp.bfloat16)


def project(parts, me, table, scales, weights, unit):
    count = len(parts)
    rows, width = parts[0].shape
    features = scales.shape[1]
    tables = [] if table is None else [table]
    return pl.pallas_call(
        functools.partial(project_kernel, count, unit, table is not None),
        out_shape=(
            jax.ShapeDtypeStruct((rows // 2, features), jnp.float32),
            jax.ShapeDtypeStruct((rows // 2, features), jnp.bfloat16),
        ),
        in_specs=[SMEM] + [VMEM] * (count + len(tables) + 2),
        out_specs=(VMEM, VMEM),
        scratch_shapes=[
            pltpu.VMEM((rows, width), jnp.bfloat16),
            pltpu.VMEM((rows * width // DENSE, DENSE), jnp.bfloat16),
        ],
        compiler_params=pltpu.CompilerParams(vmem_limit_bytes=GRANT * 2**20),
        cost_estimate=cost(2 * 128 * width * features),
        name="project",
    )(me, *parts, *tables, scales, weights)


def fold_kernel(bit, me_ref, keep_ref, got_ref, value_ref, send_ref):
    half = value_ref.shape[0]
    upper = jnp.right_shift(me_ref[0], bit) & 1 == 1
    first = keep_ref[:half, :] + got_ref[:half, :].astype(jnp.float32)
    second = keep_ref[half:, :] + got_ref[half:, :].astype(jnp.float32)
    value_ref[...] = jnp.where(upper, second, first)
    send_ref[...] = jnp.where(upper, first, second).astype(jnp.bfloat16)


def fold(keep, got, me, bit):
    rows, features = keep.shape
    return pl.pallas_call(
        functools.partial(fold_kernel, bit),
        out_shape=(
            jax.ShapeDtypeStruct((rows // 2, features), jnp.float32),
            jax.ShapeDtypeStruct((rows // 2, features), jnp.bfloat16),
        ),
        in_specs=[SMEM, VMEM, VMEM],
        out_specs=(VMEM, VMEM),
        compiler_params=pltpu.CompilerParams(vmem_limit_bytes=4 * 2**20),
        cost_estimate=cost(rows * features),
        name="fold",
    )(me, keep, got)


def finish_kernel(sizes, scale, *refs):
    chunks = len(sizes)
    keeps, gots = refs[:chunks], refs[chunks : 2 * chunks]
    residual_ref, new_ref, normed_ref = refs[2 * chunks :]
    start = 0
    for chunk, size in enumerate(sizes):
        rows = pl.ds(start, size)
        start += size
        branch = (keeps[chunk][...] + gots[chunk][...].astype(jnp.float32)) * scale
        fresh = (residual_ref[rows, :].astype(jnp.float32) + branch).astype(jnp.bfloat16)
        new_ref[rows, :] = fresh
        values = fresh.astype(jnp.float32)
        inverse = lax.rsqrt(jnp.mean(values * values, axis=1, keepdims=True) + 1e-05)
        normed_ref[rows, :] = (values * inverse).astype(jnp.bfloat16)


def finish(keeps, gots, residual, scale):
    chunks = len(keeps)
    shape = jax.ShapeDtypeStruct(residual.shape, jnp.bfloat16)
    return pl.pallas_call(
        functools.partial(finish_kernel, [keep.shape[0] for keep in keeps], scale),
        out_shape=(shape, shape),
        in_specs=[VMEM] * (2 * chunks + 1),
        out_specs=(VMEM, VMEM),
        compiler_params=pltpu.CompilerParams(vmem_limit_bytes=12 * 2**20),
        cost_estimate=cost(residual.size * 1024),
        name="finish",
    )(*keeps, *gots, residual)


def local(hidden, signs, packed, group_scales, residual):
    groups = lax.axis_size("tensor")
    bits = groups.bit_length() - 1
    me = lax.axis_index("tensor")
    where = me.reshape(1)
    total_width = hidden.shape[1] * groups
    sizes = chunk_rows(residual.shape[0])
    chunks = len(sizes)
    unit = 1.0 / math.sqrt(total_width)
    table = jnp.asarray(dense_table(), jnp.bfloat16)

    def swap(value, bit):
        return lax.ppermute(value, "tensor", [(i, i ^ (1 << bit)) for i in range(groups)])

    def bit_of(bit):
        return jnp.right_shift(me, bit) & 1

    places = [(sum(sizes[:chunk]), sizes[chunk]) for chunk in range(chunks)]
    opened = open_exchange(hidden, signs, groups, sizes[0])
    have = {0: opened}
    for bit in reversed(range(1, bits)):
        have.update({r ^ (1 << bit): swap(value, bit) for r, value in list(have.items())})
    if chunks == 1:
        have.update({r ^ 1: swap(value, 0) for r, value in list(have.items())})
        pairs = []
    else:
        other = swap(hidden, 0)
        other_signs = swap(signs, 0)
        first, *pairs = rotate(hidden, signs, other, other_signs, where, table, groups, places)
        have.update({r ^ 1: swap(value, 0) for r, value in list(have.items()) if r})
        have[1] = first
    stages = [([have[r] for r in range(groups)], table)]
    for chunk in range(1, chunks):
        keep, send = pairs[2 * chunk - 2], pairs[2 * chunk - 1]
        for bit in range(1, bits):
            got = swap(send, bit)
            if bit < bits - 1:
                keep = sign_of(bit_of(bit)) * keep + got.astype(jnp.float32)
                send = keep.astype(jnp.bfloat16)
        stages.append(([keep, got], None))
    weights = dequantize(packed, group_scales.shape[0])
    words = packed.shape[1]
    side = jnp.arange(group_scales.shape[1]) // words % 2
    scales = group_scales.astype(jnp.float32) * jnp.where(side == 1, 0.0625, 1.0)[None, :]
    scales = scales.astype(jnp.bfloat16)
    keeps, gots = [], []
    for parts, maybe_table in stages:
        value, send = project(parts, where, maybe_table, scales, weights, unit)
        got = swap(send, 0)
        for bit in range(1, bits):
            value, send = fold(value, got, where, bit)
            got = swap(send, bit)
        keeps.append(value)
        gots.append(got)
    return finish(keeps, gots, residual, 1.0 / (45.0 * math.sqrt(total_width)))


def solution(mesh):
    return jax.shard_map(
        local,
        mesh=mesh,
        in_specs=(
            P("dp", "tensor"),
            P("tensor"),
            P("tensor", None),
            P("tensor", None),
            P(("dp", "tensor"), None),
        ),
        out_specs=(P(("dp", "tensor"), None), P(("dp", "tensor"), None)),
        check_vma=False,
    )
```

profile of v0, /device:TPU:0, one launch (start us, length us, event | category | flops | bytes accessed | tf_op | source)
XLA Modules:
  0.0 73.1 jit_solution(3523508331518133405)
XLA Ops:
  0.6 0.0 copy-start
  0.6 0.0 copy-start.3
  0.6 0.6 collective-permute-start
  1.2 0.1 collective-permute-start.1
  1.3 1.2 %open_exchange.1.refs_0_ = bf16[64,3584]{1,0:T(8,128)(2,1)S(1)} custom-call(bf16[256,3584]{1,0:T(8,128)(2,1)} %hidden_ref.3, s32[3584]{0:T(1024)} %signs_ref.3), custom_call_target="tpu_custom_call" | custom-call | flops 229376 | tf_op jit(solution)/shard_map/open_exchange/pallas_call | solution.py:91
  2.5 3.0 %collective-permute-start.2 = (bf16[64,3584]{1,0:T(8,128)(2,1)S(1)}, bf16[64,3584]{1,0:T(8,128)(2,1)S(1)}, u32[]{:S(2)}, u32[]{:S(2)}) collective-permute-start(bf16[64,3584]{1,0:T(8,128)(2,1)S(1)} %open_exchange.1.refs_0_), channel_id=1, source_target_pairs={{0,2},{1,3},{2,0},{3,1},{4,6},{5,7},{6,4},{7,5},{8,10},{9,11},{10,... | collective-permute-start | bytes 1376264 | tf_op jit(solution)/shard_map/ppermute | solution.py:343
  5.5 0.0 collective-permute-done.1.other_signs_ref
  5.5 0.0 collective-permute-done.other_ref
  5.5 0.0 copy-done
  5.5 0.0 copy-done.3
  5.5 0.0 copy-start.4
  5.6 4.2 %rotate.1 = (bf16[64,3584]{1,0:T(8,128)(2,1)S(1)}, f32[128,3584]{1,0:T(8,128)S(1)}, bf16[128,3584]{1,0:T(8,128)(2,1)S(1)}, f32[64,3584]{1,0:T(8,128)S(1)}, bf16[64,3584]{1,0:T(8,128)(2,1)S(1)}) custom-call(s32[1]{0:T(128)} %bitcast.me_ref, bf16[256,3584]{1,0:T(8,128)(2,1)S(1)} %copy-done, s32[3584]{0:T(1024)S(1)} %copy-done.3, ...), custom_call_target="tpu_custom_call" | custom-call | flops 1233125376 | tf_op jit(solution)/shard_map/rotate/pallas_call | solution.py:164
  9.7 2.4 %collective-permute-start.5 = (bf16[128,3584]{1,0:T(8,128)(2,1)S(1)}, bf16[128,3584]{1,0:T(8,128)(2,1)S(1)}, u32[]{:S(2)}, u32[]{:S(2)}) collective-permute-start(bf16[128,3584]{1,0:T(8,128)(2,1)S(1)} %get-tuple-element.24), channel_id=1, source_target_pairs={{0,2},{1,3},{2,0},{3,1},{4,6},{5,7},{6,4},{7,5},{8,10},{9,11},{10,... | collective-permute-start | bytes 2752520 | tf_op jit(solution)/shard_map/ppermute | solution.py:343
  12.1 0.0 copy-done.4
  12.1 0.1 multiply_convert_fusion.refs_5_.refs_2_
  12.1 4.7 %collective-permute-done.2.refs_2_ = bf16[64,3584]{1,0:T(8,128)(2,1)S(1)} collective-permute-done((bf16[64,3584]{1,0:T(8,128)(2,1)S(1)}, bf16[64,3584]{1,0:T(8,128)(2,1)S(1)}, u32[]{:S(2)}, u32[]{:S(2)}) %collective-permute-start.2) | collective-permute-done | bytes 458784 | tf_op jit(solution)/shard_map/ppermute | solution.py:343
  16.9 0.0 collective-permute-start.3
  16.9 5.6 %dequantize.1.refs_6_.refs_3_ = s8[4,3584,512]{2,1,0:T(32,128)(4,1)S(1)} custom-call(s32[3584,512]{1,0:T(8,128)} %packed_ref.1), custom_call_target="tpu_custom_call" | custom-call | flops 7516192768 | tf_op jit(solution)/shard_map/dequantize/pallas_call | solution.py:186
  22.4 2.1 %collective-permute-start.7 = (bf16[64,3584]{1,0:T(8,128)(2,1)S(1)}, bf16[64,3584]{1,0:T(8,128)(2,1)S(1)}, u32[]{:S(2)}, u32[]{:S(2)}) collective-permute-start(bf16[64,3584]{1,0:T(8,128)(2,1)S(1)} %get-tuple-element.29), channel_id=1, source_target_pairs={{0,2},{1,3},{2,0},{3,1},{4,6},{5,7},{6,4},{7,5},{8,10},{9,11},{10,... | collective-permute-start | bytes 1376264 | tf_op jit(solution)/shard_map/ppermute | solution.py:343
  24.5 12.0 %collective-permute-done.5.refs_1_ = bf16[128,3584]{1,0:T(8,128)(2,1)S(1)} collective-permute-done((bf16[128,3584]{1,0:T(8,128)(2,1)S(1)}, bf16[128,3584]{1,0:T(8,128)(2,1)S(1)}, u32[]{:S(2)}, u32[]{:S(2)}) %collective-permute-start.5) | collective-permute-done | bytes 917536 | tf_op jit(solution)/shard_map/ppermute | solution.py:343
  36.5 0.0 copy-start.1
  36.5 6.2 %project.4 = (f32[64,4096]{1,0:T(8,128)S(1)}, bf16[64,4096]{1,0:T(8,128)(2,1)S(1)}) custom-call(s32[1]{0:T(128)} %bitcast.me_ref, f32[128,3584]{1,0:T(8,128)S(1)} %get-tuple-element.23.refs_0_, bf16[128,3584]{1,0:T(8,128)(2,1)S(1)} %collective-permute-done.5.refs_1_, bf16[28,4096]{1,0:T(8,128)(2,1)S(1)} %multiply_convert_fusion.refs_5_.refs_2_, ...), custom_call_target="tpu_custom_call" | custom-call | flops 3758096384 | tf_op jit(solution)/shard_map/project/pallas_call | solution.py:258
  42.8 0.1 collective-permute-start.6
  42.8 0.0 collective-permute-done.3.refs_3_
  42.9 0.0 copy-done.1
  42.9 7.2 %project.3 = (f32[32,4096]{1,0:T(8,128)S(1)}, bf16[32,4096]{1,0:T(8,128)(2,1)S(1)}) custom-call(s32[1]{0:T(128)} %bitcast.me_ref, bf16[64,3584]{1,0:T(8,128)(2,1)S(1)} %open_exchange.1.refs_0_, bf16[64,3584]{1,0:T(8,128)(2,1)S(1)} %get-tuple-element.19.refs_1_, bf16[64,3584]{1,0:T(8,128)(2,1)S(1)} %collective-permute-done.2.refs_2_, ...), custom_call_target="tpu_custom_call" | custom-call | flops 3758096384 | tf_op jit(solution)/shard_map/project/pallas_call | solution.py:258
  50.1 0.5 collective-permute-start.4
  50.6 0.0 collective-permute-done.7.refs_1_
  50.6 6.3 %project.5 = (f32[32,4096]{1,0:T(8,128)S(1)}, bf16[32,4096]{1,0:T(8,128)(2,1)S(1)}) custom-call(s32[1]{0:T(128)} %bitcast.me_ref, f32[64,3584]{1,0:T(8,128)S(1)} %get-tuple-element.28.refs_0_, bf16[64,3584]{1,0:T(8,128)(2,1)S(1)} %collective-permute-done.7.refs_1_, bf16[28,4096]{1,0:T(8,128)(2,1)S(1)} %multiply_convert_fusion.refs_5_.refs_2_, ...), custom_call_target="tpu_custom_call" | custom-call | flops 3758096384 | tf_op jit(solution)/shard_map/project/pallas_call | solution.py:258
  57.0 0.0 copy-start.2
  57.0 0.1 collective-permute-start.8
  57.1 0.0 collective-permute-done.6.got_ref
  57.1 0.1 fold.4
  57.2 2.1 %collective-permute-start.10 = (bf16[32,4096]{1,0:T(8,128)(2,1)S(1)}, bf16[32,4096]{1,0:T(8,128)(2,1)S(1)}, u32[]{:S(2)}, u32[]{:S(2)}) collective-permute-start(bf16[32,4096]{1,0:T(8,128)(2,1)S(1)} %get-tuple-element.34), channel_id=1, source_target_pairs={{0,2},{1,3},{2,0},{3,1},{4,6},{5,7},{6,4},{7,5},{8,10},{9,11},{10,... | collective-permute-start | bytes 786440 | tf_op jit(solution)/shard_map/ppermute | solution.py:343
  59.3 0.0 collective-permute-done.4.got_ref
  59.3 0.1 fold.3
  59.4 0.1 collective-permute-start.9
  59.4 0.0 collective-permute-done.8.got_ref
  59.4 0.1 fold.5
  59.5 2.1 %collective-permute-start.11 = (bf16[16,4096]{1,0:T(8,128)(2,1)S(1)}, bf16[16,4096]{1,0:T(8,128)(2,1)S(1)}, u32[]{:S(2)}, u32[]{:S(2)}) collective-permute-start(bf16[16,4096]{1,0:T(8,128)(2,1)S(1)} %get-tuple-element.35), channel_id=1, source_target_pairs={{0,2},{1,3},{2,0},{3,1},{4,6},{5,7},{6,4},{7,5},{8,10},{9,11},{10,... | collective-permute-start | bytes 393224 | tf_op jit(solution)/shard_map/ppermute | solution.py:343
  61.6 7.7 %collective-permute-done.9.refs_3_ = bf16[16,4096]{1,0:T(8,128)(2,1)S(1)} collective-permute-done((bf16[16,4096]{1,0:T(8,128)(2,1)S(1)}, bf16[16,4096]{1,0:T(8,128)(2,1)S(1)}, u32[]{:S(2)}, u32[]{:S(2)}) %collective-permute-start.9) | collective-permute-done | bytes 131104 | tf_op jit(solution)/shard_map/ppermute | solution.py:343
  69.3 2.6 %collective-permute-done.11.refs_5_ = bf16[16,4096]{1,0:T(8,128)(2,1)S(1)} collective-permute-done((bf16[16,4096]{1,0:T(8,128)(2,1)S(1)}, bf16[16,4096]{1,0:T(8,128)(2,1)S(1)}, u32[]{:S(2)}, u32[]{:S(2)}) %collective-permute-start.11) | collective-permute-done | bytes 131104 | tf_op jit(solution)/shard_map/ppermute | solution.py:343
  71.8 0.0 collective-permute-done.10.refs_4_
  71.9 0.0 copy-done.2
  71.9 1.2 %finish.1 = (bf16[64,4096]{1,0:T(8,128)(2,1)}, bf16[64,4096]{1,0:T(8,128)(2,1)}) custom-call(f32[16,4096]{1,0:T(8,128)S(1)} %get-tuple-element.22.refs_0_, f32[32,4096]{1,0:T(8,128)S(1)} %get-tuple-element.27.refs_1_, f32[16,4096]{1,0:T(8,128)S(1)} %get-tuple-element.32.refs_2_, bf16[16,4096]{1,0:T(8,128)(2,1)S(1)} %collective-permute-done.9.refs_3_, ...), custom_call_target="tpu_custom_call" | custom-call | flops 268435456 | tf_op jit(solution)/shard_map/finish/pallas_call | solution.py:320
  (1 shorter events, 0.0 us)
Async XLA Ops:
  0.6 4.9 %copy-start = (bf16[256,3584]{1,0:T(8,128)(2,1)S(1)}, bf16[256,3584]{1,0:T(8,128)(2,1)}, u32[]{:S(2)}) copy-start(bf16[256,3584]{1,0:T(8,128)(2,1)} %hidden_ref.3) | copy-start | bytes 5505028
  0.6 4.9 %copy-start.3 = (s32[3584]{0:T(1024)S(1)}, s32[3584]{0:T(1024)}, u32[]{:S(2)}) copy-start(s32[3584]{0:T(1024)} %signs_ref.3) | copy-start | bytes 43012
  0.6 4.9 %collective-permute-start = (bf16[256,3584]{1,0:T(8,128)(2,1)}, bf16[256,3584]{1,0:T(8,128)(2,1)}, u32[]{:S(2)}, u32[]{:S(2)}) collective-permute-start(bf16[256,3584]{1,0:T(8,128)(2,1)} %hidden_ref.3), channel_id=1, source_target_pairs={{0,1},{1,0},{2,3},{3,2},{4,5},{5,4},{6,7},{7,6},{8,9},{9,8},{10,11... | collective-permute-start | bytes 5505032 | tf_op jit(solution)/shard_map/ppermute | solution.py:343
  1.2 4.3 %collective-permute-start.1 = (s32[3584]{0:T(1024)}, s32[3584]{0:T(1024)S(1)}, u32[]{:S(2)}, u32[]{:S(2)}) collective-permute-start(s32[3584]{0:T(1024)} %signs_ref.3), channel_id=1, source_target_pairs={{0,1},{1,0},{2,3},{3,2},{4,5},{5,4},{6,7},{7,6},{8,9},{9,8},{10,11... | collective-permute-start | bytes 43016 | tf_op jit(solution)/shard_map/ppermute | solution.py:343
  2.5 14.4 %collective-permute-start.2 = (bf16[64,3584]{1,0:T(8,128)(2,1)S(1)}, bf16[64,3584]{1,0:T(8,128)(2,1)S(1)}, u32[]{:S(2)}, u32[]{:S(2)}) collective-permute-start(bf16[64,3584]{1,0:T(8,128)(2,1)S(1)} %open_exchange.1.refs_0_), channel_id=1, source_target_pairs={{0,2},{1,3},{2,0},{3,1},{4,6},{5,7},{6,4},{7,5},{8,10},{9,11},{10,... | collective-permute-start | bytes 1376264 | tf_op jit(solution)/shard_map/ppermute | solution.py:343
  5.5 6.5 %copy-start.4 = (s32[28,4096]{1,0:T(8,128)S(1)}, s32[28,4096]{1,0:T(8,128)}, u32[]{:S(2)}) copy-start(s32[28,4096]{1,0:T(8,128)} %param.9) | copy-start | bytes 1376260
  9.7 26.8 %collective-permute-start.5 = (bf16[128,3584]{1,0:T(8,128)(2,1)S(1)}, bf16[128,3584]{1,0:T(8,128)(2,1)S(1)}, u32[]{:S(2)}, u32[]{:S(2)}) collective-permute-start(bf16[128,3584]{1,0:T(8,128)(2,1)S(1)} %get-tuple-element.24), channel_id=1, source_target_pairs={{0,2},{1,3},{2,0},{3,1},{4,6},{5,7},{6,4},{7,5},{8,10},{9,11},{10,... | collective-permute-start | bytes 2752520 | tf_op jit(solution)/shard_map/ppermute | solution.py:343
  16.9 26.0 %collective-permute-start.3 = (bf16[64,3584]{1,0:T(8,128)(2,1)S(1)}, bf16[64,3584]{1,0:T(8,128)(2,1)S(1)}, u32[]{:S(2)}, u32[]{:S(2)}) collective-permute-start(bf16[64,3584]{1,0:T(8,128)(2,1)S(1)} %collective-permute-done.2.refs_2_), channel_id=1, source_target_pairs={{0,1},{1,0},{2,3},{3,2},{4,5},{5,4},{6,7},{7,6},{8,9},{9,8},{10,11... | collective-permute-start | bytes 1376264 | tf_op jit(solution)/shard_map/ppermute | solution.py:343
  22.4 28.2 %collective-permute-start.7 = (bf16[64,3584]{1,0:T(8,128)(2,1)S(1)}, bf16[64,3584]{1,0:T(8,128)(2,1)S(1)}, u32[]{:S(2)}, u32[]{:S(2)}) collective-permute-start(bf16[64,3584]{1,0:T(8,128)(2,1)S(1)} %get-tuple-element.29), channel_id=1, source_target_pairs={{0,2},{1,3},{2,0},{3,1},{4,6},{5,7},{6,4},{7,5},{8,10},{9,11},{10,... | collective-permute-start | bytes 1376264 | tf_op jit(solution)/shard_map/ppermute | solution.py:343
  36.5 6.3 %copy-start.1 = (bf16[896,896]{1,0:T(8,128)(2,1)S(1)}, bf16[896,896]{1,0:T(8,128)(2,1)}, u32[]{:S(2)}) copy-start(bf16[896,896]{1,0:T(8,128)(2,1)} %constant.42.clone.table_ref.refs_4_) | copy-start | bytes 4816900
  42.8 14.3 %collective-permute-start.6 = (bf16[64,4096]{1,0:T(8,128)(2,1)S(1)}, bf16[64,4096]{1,0:T(8,128)(2,1)S(1)}, u32[]{:S(2)}, u32[]{:S(2)}) collective-permute-start(bf16[64,4096]{1,0:T(8,128)(2,1)S(1)} %get-tuple-element.26), channel_id=1, source_target_pairs={{0,1},{1,0},{2,3},{3,2},{4,5},{5,4},{6,7},{7,6},{8,9},{9,8},{10,11... | collective-permute-start | bytes 1572872 | tf_op jit(solution)/shard_map/ppermute | solution.py:343
  50.1 9.2 %collective-permute-start.4 = (bf16[32,4096]{1,0:T(8,128)(2,1)S(1)}, bf16[32,4096]{1,0:T(8,128)(2,1)S(1)}, u32[]{:S(2)}, u32[]{:S(2)}) collective-permute-start(bf16[32,4096]{1,0:T(8,128)(2,1)S(1)} %get-tuple-element.21), channel_id=1, source_target_pairs={{0,1},{1,0},{2,3},{3,2},{4,5},{5,4},{6,7},{7,6},{8,9},{9,8},{10,11... | collective-permute-start | bytes 786440 | tf_op jit(solution)/shard_map/ppermute | solution.py:343
  57.0 14.9 %copy-start.2 = (bf16[64,4096]{1,0:T(8,128)(2,1)S(1)}, bf16[64,4096]{1,0:T(8,128)(2,1)}, u32[]{:S(2)}) copy-start(bf16[64,4096]{1,0:T(8,128)(2,1)} %refs_6_.1) | copy-start | bytes 1572868
  57.0 2.5 %collective-permute-start.8 = (bf16[32,4096]{1,0:T(8,128)(2,1)S(1)}, bf16[32,4096]{1,0:T(8,128)(2,1)S(1)}, u32[]{:S(2)}, u32[]{:S(2)}) collective-permute-start(bf16[32,4096]{1,0:T(8,128)(2,1)S(1)} %get-tuple-element.31), channel_id=1, source_target_pairs={{0,1},{1,0},{2,3},{3,2},{4,5},{5,4},{6,7},{7,6},{8,9},{9,8},{10,11... | collective-permute-start | bytes 786440 | tf_op jit(solution)/shard_map/ppermute | solution.py:343
  57.2 14.6 %collective-permute-start.10 = (bf16[32,4096]{1,0:T(8,128)(2,1)S(1)}, bf16[32,4096]{1,0:T(8,128)(2,1)S(1)}, u32[]{:S(2)}, u32[]{:S(2)}) collective-permute-start(bf16[32,4096]{1,0:T(8,128)(2,1)S(1)} %get-tuple-element.34), channel_id=1, source_target_pairs={{0,2},{1,3},{2,0},{3,1},{4,6},{5,7},{6,4},{7,5},{8,10},{9,11},{10,... | collective-permute-start | bytes 786440 | tf_op jit(solution)/shard_map/ppermute | solution.py:343
  59.4 9.9 %collective-permute-start.9 = (bf16[16,4096]{1,0:T(8,128)(2,1)S(1)}, bf16[16,4096]{1,0:T(8,128)(2,1)S(1)}, u32[]{:S(2)}, u32[]{:S(2)}) collective-permute-start(bf16[16,4096]{1,0:T(8,128)(2,1)S(1)} %get-tuple-element.33), channel_id=1, source_target_pairs={{0,2},{1,3},{2,0},{3,1},{4,6},{5,7},{6,4},{7,5},{8,10},{9,11},{10,... | collective-permute-start | bytes 393224 | tf_op jit(solution)/shard_map/ppermute | solution.py:343
  59.5 12.3 %collective-permute-start.11 = (bf16[16,4096]{1,0:T(8,128)(2,1)S(1)}, bf16[16,4096]{1,0:T(8,128)(2,1)S(1)}, u32[]{:S(2)}, u32[]{:S(2)}) collective-permute-start(bf16[16,4096]{1,0:T(8,128)(2,1)S(1)} %get-tuple-element.35), channel_id=1, source_target_pairs={{0,2},{1,3},{2,0},{3,1},{4,6},{5,7},{6,4},{7,5},{8,10},{9,11},{10,... | collective-permute-start | bytes 393224 | tf_op jit(solution)/shard_map/ppermute | solution.py:343
where the time goes:
time: 73.3 us; the launch traced here: 73.1 us
  Pallas kernels  32.2 us (44%)
  waiting for transfers between devices  27 us (37%)
  starting transfers between devices  13 us (18%)
  between operations  0.77 us (1%)
    ppermute x12, waiting for transfers between devices, swap(): lax.ppermute(value, 'tensor', [(i, i ^ 1 << bit) for i in range(groups)])  27 us
    pallas_call x3, Pallas kernels, project(): pl.pallas_call(functools.partial(project_kernel, count, unit, table is no...  19.8 us
    ppermute x12, starting transfers between devices, swap(): lax.ppermute(value, 'tensor', [(i, i ^ 1 << bit) for i in range(groups)])  13 us
    pallas_call x1, Pallas kernels, dequantize(): pl.pallas_call(dequantize_kernel, grid=(width // rows,), out_shape=jax.Sh...  5.56 us
    pallas_call x1, Pallas kernels, rotate(): pl.pallas_call(functools.partial(rotate_kernel, groups, places), out_shap...  4.15 us
  transfers between devices with their start and end apart: 12, of which 4 were waited for; matrix products, arithmetic and copies ran while one was open for 0% of the time, Pallas kernels for 42%

commit v1 on v0

--- a/solution.py
+++ b/solution.py
@@ -227,7 +227,7 @@
     half = rows // 2
     upper = me & 1 == 1
 
-    @pl.loop(0, BYTES, unroll=2)
+    @pl.loop(0, BYTES, unroll=BYTES)
     def _(place):
         spans = [
             pl.ds(pl.multiple_of((2 * place + side) * words, words), words) for side in range(2)
@@ -298,34 +298,51 @@
     )(me, keep, got)
 
 
-def finish_kernel(sizes, scale, *refs):
+def finish_kernel(start, sizes, scale, *refs):
     chunks = len(sizes)
-    keeps, gots = refs[:chunks], refs[chunks : 2 * chunks]
-    residual_ref, new_ref, normed_ref = refs[2 * chunks :]
-    start = 0
+    keeps, gots, residual_ref = refs[:chunks], refs[chunks : 2 * chunks], refs[2 * chunks]
+    new_ref, normed_ref, new_rows, normed_rows, sems = refs[-5:]
+    copies, at = [], 0
     for chunk, size in enumerate(sizes):
-        rows = pl.ds(start, size)
-        start += size
+        rows, target = pl.ds(at, size), pl.ds(start + at, size)
         branch = (keeps[chunk][...] + gots[chunk][...].astype(jnp.float32)) * scale
-        fresh = (residual_ref[rows, :].astype(jnp.float32) + branch).astype(jnp.bfloat16)
-        new_ref[rows, :] = fresh
+        fresh = (residual_ref[target, :].astype(jnp.float32) + branch).astype(jnp.bfloat16)
+        new_rows[rows, :] = fresh
         values = fresh.astype(jnp.float32)
         inverse = lax.rsqrt(jnp.mean(values * values, axis=1, keepdims=True) + 1e-05)
-        normed_ref[rows, :] = (values * inverse).astype(jnp.bfloat16)
-
-
-def finish(keeps, gots, residual, scale):
+        normed_rows[rows, :] = (values * inverse).astype(jnp.bfloat16)
+        at += size
+    span, target = pl.ds(0, at), pl.ds(start, at)
+    copies.append(pltpu.make_async_copy(new_rows.at[span, :], new_ref.at[target, :], sems.at[0]))
+    copies.append(
+        pltpu.make_async_copy(normed_rows.at[span, :], normed_ref.at[target, :], sems.at[1])
+    )
+    for copy in copies:
+        copy.start()
+    for copy in copies:
+        copy.wait()
+
+
+def finish(keeps, gots, residual, scale, start, begun):
     chunks = len(keeps)
-    shape = jax.ShapeDtypeStruct(residual.shape, jnp.bfloat16)
-    return pl.pallas_call(
-        functools.partial(finish_kernel, [keep.shape[0] for keep in keeps], scale),
+    sizes = [keep.shape[0] for keep in keeps]
+    features = residual.shape[1]
+    shape = pltpu.HBM(residual.shape, jnp.bfloat16)
+    return pl.pallas_call(
+        functools.partial(finish_kernel, start, sizes, scale),
         out_shape=(shape, shape),
-        in_specs=[VMEM] * (2 * chunks + 1),
-        out_specs=(VMEM, VMEM),
-        compiler_params=pltpu.CompilerParams(vmem_limit_bytes=12 * 2**20),
-        cost_estimate=cost(residual.size * 1024),
+        in_specs=[VMEM] * (2 * chunks + 1) + [HBM] * len(begun),
+        out_specs=(HBM, HBM),
+        input_output_aliases={2 * chunks + 1 + i: i for i in range(len(begun))},
+        scratch_shapes=[
+            pltpu.VMEM((sum(sizes), features), jnp.bfloat16),
+            pltpu.VMEM((sum(sizes), features), jnp.bfloat16),
+            pltpu.SemaphoreType.DMA((2,)),
+        ],
+        compiler_params=pltpu.CompilerParams(vmem_limit_bytes=8 * 2**20),
+        cost_estimate=cost(residual.size * 64),
         name="finish",
-    )(*keeps, *gots, residual)
+    )(*keeps, *gots, residual, *begun)
 
 
 def local(hidden, signs, packed, group_scales, residual):
@@ -382,7 +399,12 @@
             got = swap(send, bit)
         keeps.append(value)
         gots.append(got)
-    return finish(keeps, gots, residual, 1.0 / (45.0 * math.sqrt(total_width)))
+    scale = 1.0 / (45.0 * math.sqrt(total_width))
+    begun = []
+    if chunks > 1:
+        begun = finish(keeps[:-1], gots[:-1], residual, scale, 0, [])
+    begun = finish(keeps[-1:], gots[-1:], residual, scale, sum(sizes[:-1]), begun)
+    return tuple(begun)
 
 
 def solution(mesh):

time: 73.3 us -> 71.3 us (0.973)
  waiting for transfers between devices: 27 us -> 25.7 us
  Pallas kernels: 32.2 us -> 31.4 us
    pallas_call x3, Pallas kernels: 19.8 us -> 18 us  [project(): pl.pallas_call(functools.partial(project_kernel, count, unit, table is no...]
    ppermute x12, waiting for transfers between devices: 27 us -> 25.7 us  [swap(): lax.ppermute(value, 'tensor', [(i, i ^ 1 << bit) for i in range(groups)])]
    pallas_call x1 -> x2, Pallas kernels: 1.23 us -> 1.95 us  [finish(): pl.pallas_call(functools.partial(finish_kernel, start, sizes, scale), out...]
  transfers between devices with their start and end apart: 12 -> 12, of which waited for: 4 -> 4; matrix products, arithmetic and copies ran while one was open for 0% -> 0% of each run, Pallas kernels for 42% -> 43%
where the time goes in v1:
time: 71.3 us; the launch traced here: 71.1 us
  Pallas kernels  31.4 us (44%)
  waiting for transfers between devices  25.7 us (36%)
  starting transfers between devices  13 us (18%)
  between operations  0.96 us (1%)
    ppermute x12, waiting for transfers between devices, swap(): lax.ppermute(value, 'tensor', [(i, i ^ 1 << bit) for i in range(groups)])  25.7 us
    pallas_call x3, Pallas kernels, project(): pl.pallas_call(functools.partial(project_kernel, count, unit, table is no...  18 us
    ppermute x12, starting transfers between devices, swap(): lax.ppermute(value, 'tensor', [(i, i ^ 1 << bit) for i in range(groups)])  13 us
    pallas_call x1, Pallas kernels, dequantize(): pl.pallas_call(dequantize_kernel, grid=(width // rows,), out_shape=jax.Sh...  5.74 us
    pallas_call x1, Pallas kernels, rotate(): pl.pallas_call(functools.partial(rotate_kernel, groups, places), out_shap...  4.15 us
    pallas_call x2, Pallas kernels, finish(): pl.pallas_call(functools.partial(finish_kernel, start, sizes, scale), out...  1.95 us
  transfers between devices with their start and end apart: 12, of which 4 were waited for; matrix products, arithmetic and copies ran while one was open for 0% of the time, Pallas kernels for 43%

profile of v1, /device:TPU:0, one launch (start us, length us, event | category | flops | bytes accessed | tf_op | source)
XLA Modules:
  0.0 71.1 jit_solution(9976066591233135458)
XLA Ops:
  0.6 0.0 copy-start
  0.6 0.0 copy-start.3
  0.6 0.6 collective-permute-start
  1.2 0.1 collective-permute-start.1
  1.3 1.2 %open_exchange.1.refs_0_ = bf16[64,3584]{1,0:T(8,128)(2,1)S(1)} custom-call(bf16[256,3584]{1,0:T(8,128)(2,1)} %hidden_ref.3, s32[3584]{0:T(1024)} %signs_ref.3), custom_call_target="tpu_custom_call" | custom-call | flops 229376 | tf_op jit(solution)/shard_map/open_exchange/pallas_call | solution.py:91
  2.5 3.0 %collective-permute-start.5 = (bf16[64,3584]{1,0:T(8,128)(2,1)S(1)}, bf16[64,3584]{1,0:T(8,128)(2,1)S(1)}, u32[]{:S(2)}, u32[]{:S(2)}) collective-permute-start(bf16[64,3584]{1,0:T(8,128)(2,1)S(1)} %open_exchange.1.refs_0_), channel_id=1, source_target_pairs={{0,2},{1,3},{2,0},{3,1},{4,6},{5,7},{6,4},{7,5},{8,10},{9,11},{10,... | collective-permute-start | bytes 1376264 | tf_op jit(solution)/shard_map/ppermute | solution.py:360
  5.5 0.0 collective-permute-done.1.other_signs_ref
  5.5 0.0 collective-permute-done.other_ref
  5.5 0.0 copy-done
  5.5 0.0 copy-done.3
  5.5 0.0 copy-start.4
  5.6 4.2 %rotate.1 = (bf16[64,3584]{1,0:T(8,128)(2,1)S(1)}, f32[128,3584]{1,0:T(8,128)S(1)}, bf16[128,3584]{1,0:T(8,128)(2,1)S(1)}, f32[64,3584]{1,0:T(8,128)S(1)}, bf16[64,3584]{1,0:T(8,128)(2,1)S(1)}) custom-call(s32[1]{0:T(128)} %bitcast.me_ref, bf16[256,3584]{1,0:T(8,128)(2,1)S(1)} %copy-done, s32[3584]{0:T(1024)S(1)} %copy-done.3, ...), custom_call_target="tpu_custom_call" | custom-call | flops 1233125376 | tf_op jit(solution)/shard_map/rotate/pallas_call | solution.py:164
  9.7 2.4 %collective-permute-start.8 = (bf16[128,3584]{1,0:T(8,128)(2,1)S(1)}, bf16[128,3584]{1,0:T(8,128)(2,1)S(1)}, u32[]{:S(2)}, u32[]{:S(2)}) collective-permute-start(bf16[128,3584]{1,0:T(8,128)(2,1)S(1)} %get-tuple-element.32), channel_id=1, source_target_pairs={{0,2},{1,3},{2,0},{3,1},{4,6},{5,7},{6,4},{7,5},{8,10},{9,11},{10,... | collective-permute-start | bytes 2752520 | tf_op jit(solution)/shard_map/ppermute | solution.py:360
  12.1 0.0 copy-done.4
  12.1 0.1 multiply_convert_fusion.refs_2_.refs_5_
  12.1 4.7 %collective-permute-done.5.refs_2_ = bf16[64,3584]{1,0:T(8,128)(2,1)S(1)} collective-permute-done((bf16[64,3584]{1,0:T(8,128)(2,1)S(1)}, bf16[64,3584]{1,0:T(8,128)(2,1)S(1)}, u32[]{:S(2)}, u32[]{:S(2)}) %collective-permute-start.5) | collective-permute-done | bytes 458784 | tf_op jit(solution)/shard_map/ppermute | solution.py:360
  16.9 0.0 collective-permute-start.6
  16.9 5.7 %dequantize.1.refs_3_.refs_6_ = s8[4,3584,512]{2,1,0:T(32,128)(4,1)S(1)} custom-call(s32[3584,512]{1,0:T(8,128)} %packed_ref.1), custom_call_target="tpu_custom_call" | custom-call | flops 7516192768 | tf_op jit(solution)/shard_map/dequantize/pallas_call | solution.py:186
  22.6 2.1 %collective-permute-start.2 = (bf16[64,3584]{1,0:T(8,128)(2,1)S(1)}, bf16[64,3584]{1,0:T(8,128)(2,1)S(1)}, u32[]{:S(2)}, u32[]{:S(2)}) collective-permute-start(bf16[64,3584]{1,0:T(8,128)(2,1)S(1)} %get-tuple-element.22), channel_id=1, source_target_pairs={{0,2},{1,3},{2,0},{3,1},{4,6},{5,7},{6,4},{7,5},{8,10},{9,11},{10,... | collective-permute-start | bytes 1376264 | tf_op jit(solution)/shard_map/ppermute | solution.py:360
  24.7 11.8 %collective-permute-done.8.refs_1_ = bf16[128,3584]{1,0:T(8,128)(2,1)S(1)} collective-permute-done((bf16[128,3584]{1,0:T(8,128)(2,1)S(1)}, bf16[128,3584]{1,0:T(8,128)(2,1)S(1)}, u32[]{:S(2)}, u32[]{:S(2)}) %collective-permute-start.8) | collective-permute-done | bytes 917536 | tf_op jit(solution)/shard_map/ppermute | solution.py:360
  36.5 0.0 copy-start.2
  36.5 5.9 %project.5 = (f32[64,4096]{1,0:T(8,128)S(1)}, bf16[64,4096]{1,0:T(8,128)(2,1)S(1)}) custom-call(s32[1]{0:T(128)} %bitcast.me_ref, f32[128,3584]{1,0:T(8,128)S(1)} %get-tuple-element.31.refs_0_, bf16[128,3584]{1,0:T(8,128)(2,1)S(1)} %collective-permute-done.8.refs_1_, bf16[28,4096]{1,0:T(8,128)(2,1)S(1)} %multiply_convert_fusion.refs_2_.refs_5_, ...), custom_call_target="tpu_custom_call" | custom-call | flops 3758096384 | tf_op jit(solution)/shard_map/project/pallas_call | solution.py:258
  42.4 0.1 collective-permute-start.9
  42.5 0.0 collective-permute-done.6.refs_3_
  42.5 0.0 copy-done.2
  42.5 5.8 %project.4 = (f32[32,4096]{1,0:T(8,128)S(1)}, bf16[32,4096]{1,0:T(8,128)(2,1)S(1)}) custom-call(s32[1]{0:T(128)} %bitcast.me_ref, bf16[64,3584]{1,0:T(8,128)(2,1)S(1)} %open_exchange.1.refs_0_, bf16[64,3584]{1,0:T(8,128)(2,1)S(1)} %get-tuple-element.27.refs_1_, bf16[64,3584]{1,0:T(8,128)(2,1)S(1)} %collective-permute-done.5.refs_2_, ...), custom_call_target="tpu_custom_call" | custom-call | flops 3758096384 | tf_op jit(solution)/shard_map/project/pallas_call | solution.py:258
  48.3 0.5 collective-permute-start.7
  48.8 0.0 collective-permute-done.2.refs_1_
  48.8 6.4 %project.3 = (f32[32,4096]{1,0:T(8,128)S(1)}, bf16[32,4096]{1,0:T(8,128)(2,1)S(1)}) custom-call(s32[1]{0:T(128)} %bitcast.me_ref, f32[64,3584]{1,0:T(8,128)S(1)} %get-tuple-element.21.refs_0_, bf16[64,3584]{1,0:T(8,128)(2,1)S(1)} %collective-permute-done.2.refs_1_, bf16[28,4096]{1,0:T(8,128)(2,1)S(1)} %multiply_convert_fusion.refs_2_.refs_5_, ...), custom_call_target="tpu_custom_call" | custom-call | flops 3758096384 | tf_op jit(solution)/shard_map/project/pallas_call | solution.py:258
  55.2 0.0 copy-start.1
  55.2 0.1 collective-permute-start.3
  55.3 0.0 collective-permute-done.9.got_ref
  55.3 0.1 fold.5
  55.5 2.1 %collective-permute-start.11 = (bf16[32,4096]{1,0:T(8,128)(2,1)S(1)}, bf16[32,4096]{1,0:T(8,128)(2,1)S(1)}, u32[]{:S(2)}, u32[]{:S(2)}) collective-permute-start(bf16[32,4096]{1,0:T(8,128)(2,1)S(1)} %get-tuple-element.37), channel_id=1, source_target_pairs={{0,2},{1,3},{2,0},{3,1},{4,6},{5,7},{6,4},{7,5},{8,10},{9,11},{10,... | collective-permute-start | bytes 786440 | tf_op jit(solution)/shard_map/ppermute | solution.py:360
  57.6 0.0 collective-permute-done.7.got_ref
  57.6 0.1 fold.4
  57.6 0.1 collective-permute-start.10
  57.7 0.0 collective-permute-done.3.got_ref
  57.7 0.1 fold.3
  57.8 2.1 %collective-permute-start.4 = (bf16[16,4096]{1,0:T(8,128)(2,1)S(1)}, bf16[16,4096]{1,0:T(8,128)(2,1)S(1)}, u32[]{:S(2)}, u32[]{:S(2)}) collective-permute-start(bf16[16,4096]{1,0:T(8,128)(2,1)S(1)} %get-tuple-element.26), channel_id=1, source_target_pairs={{0,2},{1,3},{2,0},{3,1},{4,6},{5,7},{6,4},{7,5},{8,10},{9,11},{10,... | collective-permute-start | bytes 393224 | tf_op jit(solution)/shard_map/ppermute | solution.py:360
  59.9 7.7 %collective-permute-done.10.refs_2_ = bf16[16,4096]{1,0:T(8,128)(2,1)S(1)} collective-permute-done((bf16[16,4096]{1,0:T(8,128)(2,1)S(1)}, bf16[16,4096]{1,0:T(8,128)(2,1)S(1)}, u32[]{:S(2)}, u32[]{:S(2)}) %collective-permute-start.10) | collective-permute-done | bytes 131104 | tf_op jit(solution)/shard_map/ppermute | solution.py:360
  67.5 0.0 collective-permute-done.11.refs_3_
  67.5 0.0 copy-done.1
  67.5 1.1 %finish.2 = (bf16[64,4096]{1,0:T(8,128)(2,1)}, bf16[64,4096]{1,0:T(8,128)(2,1)}) custom-call(f32[16,4096]{1,0:T(8,128)S(1)} %get-tuple-element.30.refs_0_, f32[32,4096]{1,0:T(8,128)S(1)} %get-tuple-element.35.refs_1_, bf16[16,4096]{1,0:T(8,128)(2,1)S(1)} %collective-permute-done.10.refs_2_, bf16[32,4096]{1,0:T(8,128)(2,1)S(1)} %collective-permute-done.11.refs_3_, ...), custom_call_target="tpu_custom_call" | custom-call | flops 16777216 | tf_op jit(solution)/shard_map/finish/pallas_call | solution.py:331
  68.7 1.5 %collective-permute-done.4.refs_1_ = bf16[16,4096]{1,0:T(8,128)(2,1)S(1)} collective-permute-done((bf16[16,4096]{1,0:T(8,128)(2,1)S(1)}, bf16[16,4096]{1,0:T(8,128)(2,1)S(1)}, u32[]{:S(2)}, u32[]{:S(2)}) %collective-permute-start.4) | collective-permute-done | bytes 131104 | tf_op jit(solution)/shard_map/ppermute | solution.py:360
  70.1 0.8 %finish.3 = (bf16[64,4096]{1,0:T(8,128)(2,1)}, bf16[64,4096]{1,0:T(8,128)(2,1)}) custom-call(f32[16,4096]{1,0:T(8,128)S(1)} %get-tuple-element.25.refs_0_, bf16[16,4096]{1,0:T(8,128)(2,1)S(1)} %collective-permute-done.4.refs_1_, bf16[64,4096]{1,0:T(8,128)(2,1)S(1)} %copy-done.1, ...), custom_call_target="tpu_custom_call", output_to_operand_aliasing={{0}: (3, {}), {1}: (4, {})} | custom-call | flops 16777216 | tf_op jit(solution)/shard_map/finish/pallas_call | solution.py:331
  (1 shorter events, 0.0 us)
Async XLA Ops:
  0.6 4.9 %copy-start = (bf16[256,3584]{1,0:T(8,128)(2,1)S(1)}, bf16[256,3584]{1,0:T(8,128)(2,1)}, u32[]{:S(2)}) copy-start(bf16[256,3584]{1,0:T(8,128)(2,1)} %hidden_ref.3) | copy-start | bytes 5505028
  0.6 4.9 %copy-start.3 = (s32[3584]{0:T(1024)S(1)}, s32[3584]{0:T(1024)}, u32[]{:S(2)}) copy-start(s32[3584]{0:T(1024)} %signs_ref.3) | copy-start | bytes 43012
  0.6 4.9 %collective-permute-start = (bf16[256,3584]{1,0:T(8,128)(2,1)}, bf16[256,3584]{1,0:T(8,128)(2,1)}, u32[]{:S(2)}, u32[]{:S(2)}) collective-permute-start(bf16[256,3584]{1,0:T(8,128)(2,1)} %hidden_ref.3), channel_id=1, source_target_pairs={{0,1},{1,0},{2,3},{3,2},{4,5},{5,4},{6,7},{7,6},{8,9},{9,8},{10,11... | collective-permute-start | bytes 5505032 | tf_op jit(solution)/shard_map/ppermute | solution.py:360
  1.2 4.3 %collective-permute-start.1 = (s32[3584]{0:T(1024)}, s32[3584]{0:T(1024)S(1)}, u32[]{:S(2)}, u32[]{:S(2)}) collective-permute-start(s32[3584]{0:T(1024)} %signs_ref.3), channel_id=1, source_target_pairs={{0,1},{1,0},{2,3},{3,2},{4,5},{5,4},{6,7},{7,6},{8,9},{9,8},{10,11... | collective-permute-start | bytes 43016 | tf_op jit(solution)/shard_map/ppermute | solution.py:360
  2.5 14.4 %collective-permute-start.5 = (bf16[64,3584]{1,0:T(8,128)(2,1)S(1)}, bf16[64,3584]{1,0:T(8,128)(2,1)S(1)}, u32[]{:S(2)}, u32[]{:S(2)}) collective-permute-start(bf16[64,3584]{1,0:T(8,128)(2,1)S(1)} %open_exchange.1.refs_0_), channel_id=1, source_target_pairs={{0,2},{1,3},{2,0},{3,1},{4,6},{5,7},{6,4},{7,5},{8,10},{9,11},{10,... | collective-permute-start | bytes 1376264 | tf_op jit(solution)/shard_map/ppermute | solution.py:360
  5.5 6.5 %copy-start.4 = (s32[28,4096]{1,0:T(8,128)S(1)}, s32[28,4096]{1,0:T(8,128)}, u32[]{:S(2)}) copy-start(s32[28,4096]{1,0:T(8,128)} %param.9) | copy-start | bytes 1376260
  9.7 26.8 %collective-permute-start.8 = (bf16[128,3584]{1,0:T(8,128)(2,1)S(1)}, bf16[128,3584]{1,0:T(8,128)(2,1)S(1)}, u32[]{:S(2)}, u32[]{:S(2)}) collective-permute-start(bf16[128,3584]{1,0:T(8,128)(2,1)S(1)} %get-tuple-element.32), channel_id=1, source_target_pairs={{0,2},{1,3},{2,0},{3,1},{4,6},{5,7},{6,4},{7,5},{8,10},{9,11},{10,... | collective-permute-start | bytes 2752520 | tf_op jit(solution)/shard_map/ppermute | solution.py:360
  16.9 25.6 %collective-permute-start.6 = (bf16[64,3584]{1,0:T(8,128)(2,1)S(1)}, bf16[64,3584]{1,0:T(8,128)(2,1)S(1)}, u32[]{:S(2)}, u32[]{:S(2)}) collective-permute-start(bf16[64,3584]{1,0:T(8,128)(2,1)S(1)} %collective-permute-done.5.refs_2_), channel_id=1, source_target_pairs={{0,1},{1,0},{2,3},{3,2},{4,5},{5,4},{6,7},{7,6},{8,9},{9,8},{10,11... | collective-permute-start | bytes 1376264 | tf_op jit(solution)/shard_map/ppermute | solution.py:360
  22.6 26.2 %collective-permute-start.2 = (bf16[64,3584]{1,0:T(8,128)(2,1)S(1)}, bf16[64,3584]{1,0:T(8,128)(2,1)S(1)}, u32[]{:S(2)}, u32[]{:S(2)}) collective-permute-start(bf16[64,3584]{1,0:T(8,128)(2,1)S(1)} %get-tuple-element.22), channel_id=1, source_target_pairs={{0,2},{1,3},{2,0},{3,1},{4,6},{5,7},{6,4},{7,5},{8,10},{9,11},{10,... | collective-permute-start | bytes 1376264 | tf_op jit(solution)/shard_map/ppermute | solution.py:360
  36.5 6.0 %copy-start.2 = (bf16[896,896]{1,0:T(8,128)(2,1)S(1)}, bf16[896,896]{1,0:T(8,128)(2,1)}, u32[]{:S(2)}) copy-start(bf16[896,896]{1,0:T(8,128)(2,1)} %constant.42.clone.table_ref.refs_4_) | copy-start | bytes 4816900
  42.4 12.9 %collective-permute-start.9 = (bf16[64,4096]{1,0:T(8,128)(2,1)S(1)}, bf16[64,4096]{1,0:T(8,128)(2,1)S(1)}, u32[]{:S(2)}, u32[]{:S(2)}) collective-permute-start(bf16[64,4096]{1,0:T(8,128)(2,1)S(1)} %get-tuple-element.34), channel_id=1, source_target_pairs={{0,1},{1,0},{2,3},{3,2},{4,5},{5,4},{6,7},{7,6},{8,9},{9,8},{10,11... | collective-permute-start | bytes 1572872 | tf_op jit(solution)/shard_map/ppermute | solution.py:360
  48.3 9.3 %collective-permute-start.7 = (bf16[32,4096]{1,0:T(8,128)(2,1)S(1)}, bf16[32,4096]{1,0:T(8,128)(2,1)S(1)}, u32[]{:S(2)}, u32[]{:S(2)}) collective-permute-start(bf16[32,4096]{1,0:T(8,128)(2,1)S(1)} %get-tuple-element.29), channel_id=1, source_target_pairs={{0,1},{1,0},{2,3},{3,2},{4,5},{5,4},{6,7},{7,6},{8,9},{9,8},{10,11... | collective-permute-start | bytes 786440 | tf_op jit(solution)/shard_map/ppermute | solution.py:360
  55.2 12.3 %copy-start.1 = (bf16[64,4096]{1,0:T(8,128)(2,1)S(1)}, bf16[64,4096]{1,0:T(8,128)(2,1)}, u32[]{:S(2)}) copy-start(bf16[64,4096]{1,0:T(8,128)(2,1)} %refs_2_.1) | copy-start | bytes 1572868
  55.2 2.5 %collective-permute-start.3 = (bf16[32,4096]{1,0:T(8,128)(2,1)S(1)}, bf16[32,4096]{1,0:T(8,128)(2,1)S(1)}, u32[]{:S(2)}, u32[]{:S(2)}) collective-permute-start(bf16[32,4096]{1,0:T(8,128)(2,1)S(1)} %get-tuple-element.24), channel_id=1, source_target_pairs={{0,1},{1,0},{2,3},{3,2},{4,5},{5,4},{6,7},{7,6},{8,9},{9,8},{10,11... | collective-permute-start | bytes 786440 | tf_op jit(solution)/shard_map/ppermute | solution.py:360
  55.5 12.1 %collective-permute-start.11 = (bf16[32,4096]{1,0:T(8,128)(2,1)S(1)}, bf16[32,4096]{1,0:T(8,128)(2,1)S(1)}, u32[]{:S(2)}, u32[]{:S(2)}) collective-permute-start(bf16[32,4096]{1,0:T(8,128)(2,1)S(1)} %get-tuple-element.37), channel_id=1, source_target_pairs={{0,2},{1,3},{2,0},{3,1},{4,6},{5,7},{6,4},{7,5},{8,10},{9,11},{10,... | collective-permute-start | bytes 786440 | tf_op jit(solution)/shard_map/ppermute | solution.py:360
  57.6 9.9 %collective-permute-start.10 = (bf16[16,4096]{1,0:T(8,128)(2,1)S(1)}, bf16[16,4096]{1,0:T(8,128)(2,1)S(1)}, u32[]{:S(2)}, u32[]{:S(2)}) collective-permute-start(bf16[16,4096]{1,0:T(8,128)(2,1)S(1)} %get-tuple-element.36), channel_id=1, source_target_pairs={{0,2},{1,3},{2,0},{3,1},{4,6},{5,7},{6,4},{7,5},{8,10},{9,11},{10,... | collective-permute-start | bytes 393224 | tf_op jit(solution)/shard_map/ppermute | solution.py:360
  57.8 12.3 %collective-permute-start.4 = (bf16[16,4096]{1,0:T(8,128)(2,1)S(1)}, bf16[16,4096]{1,0:T(8,128)(2,1)S(1)}, u32[]{:S(2)}, u32[]{:S(2)}) collective-permute-start(bf16[16,4096]{1,0:T(8,128)(2,1)S(1)} %get-tuple-element.26), channel_id=1, source_target_pairs={{0,2},{1,3},{2,0},{3,1},{4,6},{5,7},{6,4},{7,5},{8,10},{9,11},{10,... | collective-permute-start | bytes 393224 | tf_op jit(solution)/shard_map/ppermute | solution.py:360
